TPU v7x, 32 devices: a whole 2x2x4 slice. The times are simulated.
32 devices in a mesh: groups: 2 (over y), seq: 4 (over z), head: 4 (over x, core).
Axes of the slice: x: 2, y: 2, z: 4, core: 2. Of those that a mesh axis runs over, the one named last changes fastest.
Arguments:
- tile_tokens: bfloat16 [16, 256, 1536], P(('groups', 'seq')), parts along dimension 0, may hold values from -6 to 6
- tile_gain: float32 [1536], replicated, may hold values from 0.1 to 1.9
- w_gate_up: bfloat16 [2, 1536, 4096], P(None, 'seq', 'head'), may hold values from -0.15625 to 0.15625
- w_down: bfloat16 [4096, 1536], P('head', 'seq'), may hold values from -0.09375 to 0.09375
- layer_scale: float32 [1536], replicated, may hold values from 1 to 8
- fc_gain: float32 [1536], replicated, may hold values from 0.1 to 1.9
- w_embed: bfloat16 [1536, 768], P(None, 'head'), may hold values from -0.15625 to 0.15625
- embed_bias: float32 [768], P('head'), may hold values from -3 to 3
- pre_emb: bfloat16 [2032, 768], P(('groups', 'seq'), 'head'), parts along dimension 0, may hold values from -6 to 6
- tile_order: int32 [2048], P('groups'), parts along dimension 0, may hold values from 0 to 1023, as said below
- valid_count: int32 [2], P('groups'), parts along dimension 0, may hold values from 256 to 1024
- slide_gain: float32 [768], replicated, may hold values from 0.1 to 1.9
- w_qkv: bfloat16 [3, 768, 768], P(None, None, 'head'), may hold values from -1.25 to 1.25
- sub_gain: float32 [768], P('head'), may hold values from 0.1 to 1.9
- w_out: bfloat16 [768, 768], P('head'), may hold values from -0.21875 to 0.21875
Outputs:
- mixed: float32 [2048, 768], P(('groups', 'seq'), 'head'), parts along dimension 0
There are 2 independent parts, one for each index of `groups`. A program takes and returns all parts, laid end to end along the dimension named above; an argument that names none is the same for every part. Nothing has to cross between parts.
Inputs may be any that keep to these rules, and one draw needn't show every extreme that they name: `tile_order`: A permutation of 0 to 1023. For every block of 256 positions (d * 256 to (d + 1) * 256 - 1) and every block of 256 stored rows, exactly 64 positions of the first take rows of the second.
All inputs are finite; a program needn't handle non-finite values.
Results may differ from a plain program's by a relative error of at most 0.0046.
Values may be sent and summed in bfloat16 or wider, within the bound.
A program may use at most 64 MiB of HBM per device.

v0:
```python
import math
import jax
import jax.numpy as jnp
from jax import lax
from jax.sharding import PartitionSpec as P

DS = 768
HEAD_DIM = 48
SPAN0 = 1024
SPAN1 = 4096
DILATION_SECOND = 4
DILATION_THIRD = 16
layer_eps = 1e-05
masked_score = -1e30


def from_partner(value, axis, bit):
    mask = 2**bit
    pairs = [(source, source ^ mask) for source in range(lax.axis_size(axis))]
    return lax.ppermute(value, axis, pairs)


def normalize(values, gain):
    centered = values - jnp.mean(values, axis=-1, keepdims=True)
    variance = jnp.mean(centered * centered, axis=-1, keepdims=True)
    return centered * lax.rsqrt(variance + layer_eps) * gain


def select_rows(stacked, dilation, offsets):
    group_count, row_count, row_width = stacked.shape
    head_count = offsets.shape[0]
    arranged = stacked.reshape(
        group_count, row_count // dilation, dilation, head_count, row_width // head_count
    )
    choose = jnp.arange(dilation, dtype=jnp.int32)[:, None] == offsets[None, :]
    chosen = jnp.sum(
        jnp.where(choose[None, None, :, :, None], arranged, jnp.zeros((), stacked.dtype)), axis=2
    )
    return chosen.reshape(group_count, row_count // dilation, row_width)


def scatter_rows(attended, log_mass, dilation, offsets):
    query_count, head_count, head_size = attended.shape
    choose = jnp.arange(dilation, dtype=jnp.int32)[:, None] == offsets[None, :]
    spread_out = jnp.where(choose[None, :, :, None], attended[:, None, :, :], 0.0).reshape(
        query_count * dilation, head_count, head_size
    )
    spread_mass = jnp.where(choose[None, :, :], log_mass[:, None, :], masked_score).reshape(
        query_count * dilation, head_count
    )
    selected = jnp.broadcast_to(choose[None, :, :], (query_count, dilation, head_count)).reshape(
        query_count * dilation, head_count
    )
    return (spread_out, spread_mass, selected)


def attend(query_rows, key_rows, value_rows, positions, valid_limit, head_count):
    head_size = query_rows.shape[1] // head_count
    query_heads = query_rows.reshape(query_rows.shape[0], head_count, head_size)
    key_heads = key_rows.reshape(key_rows.shape[0], head_count, head_size)
    value_heads = value_rows.reshape(value_rows.shape[0], head_count, head_size)
    scores = jnp.einsum(
        "qhe,khe->hqk", query_heads, key_heads, preferred_element_type=jnp.float32
    ) / math.sqrt(head_size)
    scores = jnp.where((positions < valid_limit)[:, None, :], scores, masked_score)
    highest = jnp.max(scores, axis=-1, keepdims=True)
    exponent = jnp.exp(scores - highest)
    mass_sum = jnp.sum(exponent, axis=-1, keepdims=True)
    weights = (exponent / mass_sum).astype(jnp.bfloat16)
    attended = jnp.einsum("hqk,khe->qhe", weights, value_heads, preferred_element_type=jnp.float32)
    return (attended, (highest[..., 0] + jnp.log(mass_sum[..., 0])).T)


def body(
    tile_tokens,
    tile_gain,
    w_gate_up,
    w_down,
    layer_scale,
    fc_gain,
    w_embed,
    embed_bias,
    pre_emb,
    tile_order,
    valid_count,
    slide_gain,
    w_qkv,
    sub_gain,
    w_out,
):
    new_count, patch_count, tile_width = tile_tokens.shape
    token_rows = tile_tokens.reshape(new_count * patch_count, tile_width)
    normed = normalize(token_rows.astype(jnp.float32), tile_gain).astype(jnp.bfloat16)
    hidden_width = w_gate_up.shape[2]
    gate_up = jnp.einsum(
        "rk,gkf->grf",
        normed,
        lax.all_gather(w_gate_up, "seq", axis=1, tiled=True),
        preferred_element_type=jnp.float32,
    )
    hidden = (jax.nn.silu(gate_up[0]) * gate_up[1]).astype(jnp.bfloat16)
    pooled_hidden = jnp.mean(
        hidden.reshape(new_count, patch_count, hidden_width), axis=1, dtype=jnp.float32
    )
    everyone = lax.all_gather(pooled_hidden, "seq", axis=0, tiled=True)
    local_part = jnp.dot(everyone, w_down.astype(jnp.float32), precision=lax.Precision.HIGHEST)
    pooled_part = lax.all_to_all(local_part, "seq", split_axis=0, concat_axis=1, tiled=True)
    summed = lax.psum(pooled_part, "head")
    pooled = jnp.mean(tile_tokens, axis=1, dtype=jnp.float32) + layer_scale * summed
    feature = normalize(pooled, fc_gain).astype(jnp.bfloat16)
    new_rows = (jnp.dot(feature, w_embed, preferred_element_type=jnp.float32) + embed_bias).astype(
        jnp.bfloat16
    )
    stored = jnp.concatenate([new_rows, pre_emb], axis=0)
    block_rows = stored.shape[0]
    total_rows = tile_order.shape[0]
    peer_rows = block_rows // lax.axis_size("seq")
    device = lax.axis_index("seq")
    local_index = jnp.arange(block_rows, dtype=jnp.int32)
    inverse = (
        jnp.zeros((total_rows,), jnp.int32)
        .at[tile_order]
        .set(jnp.arange(total_rows, dtype=jnp.int32))
    )
    placed = lax.dynamic_slice_in_dim(inverse, device * block_rows, block_rows)
    target = placed // block_rows
    before = (target[:, None] == target[None, :]) & (placed[None, :] < placed[:, None])
    slot_index = target * peer_rows + jnp.sum(before, axis=1, dtype=jnp.int32)
    routing = (slot_index[None, :] == local_index[:, None]).astype(jnp.bfloat16)
    outgoing = jnp.dot(routing, stored, preferred_element_type=jnp.float32).astype(jnp.bfloat16)
    incoming = lax.all_to_all(outgoing, "seq", split_axis=0, concat_axis=0, tiled=True)
    wanted = lax.dynamic_slice_in_dim(tile_order, device * block_rows, block_rows)
    source = wanted // block_rows
    earlier = (source[:, None] == source[None, :]) & (local_index[None, :] < local_index[:, None])
    arrival = source * peer_rows + jnp.sum(earlier, axis=1, dtype=jnp.int32)
    own_part = jnp.take(incoming, arrival, axis=0)
    sequence = lax.all_gather(own_part, "head", axis=1, tiled=True)
    slide_normed = normalize(sequence.astype(jnp.float32), slide_gain).astype(jnp.bfloat16)
    projected_rows = jnp.einsum(
        "rd,gdc->grc", slide_normed, w_qkv, preferred_element_type=jnp.float32
    ).astype(jnp.bfloat16)
    cols_here = projected_rows.shape[2]
    head_count = cols_here // HEAD_DIM
    head_indices = lax.axis_index("head") * head_count + jnp.arange(head_count, dtype=jnp.int32)
    valid_limit = valid_count[0]
    row_index = device * block_rows + local_index
    near_devices = min(SPAN0, total_rows) // block_rows
    near_rows = projected_rows[1:]
    for bit_index in range(near_devices.bit_length() - 1):
        partner = from_partner(near_rows, "seq", bit_index)
        upper_half = device // (1 << bit_index) % 2 == 1
        near_rows = jnp.where(
            upper_half,
            jnp.concatenate([partner, near_rows], 1),
            jnp.concatenate([near_rows, partner], 1),
        )
    near_start = device // near_devices * near_devices * block_rows
    near_pos = jnp.broadcast_to(
        near_start + jnp.arange(near_rows.shape[1], dtype=jnp.int32),
        (head_count, near_rows.shape[1]),
    )
    near_out, near_mass = attend(
        projected_rows[0], near_rows[0], near_rows[1], near_pos, valid_limit, head_count
    )
    near_sel = jnp.ones((block_rows, head_count), dtype=bool)
    middle_level_offsets = head_indices % DILATION_SECOND
    middle_level = select_rows(projected_rows, DILATION_SECOND, middle_level_offsets)
    middle_devices = min(SPAN1, total_rows) // block_rows
    middle_key_value = middle_level[1:]
    every_row = lax.all_gather(middle_key_value, "seq", axis=1, tiled=True)
    group_rows = middle_devices * middle_key_value.shape[1]
    middle_key_value = lax.dynamic_slice_in_dim(
        every_row, device // middle_devices * group_rows, group_rows, 1
    )
    middle_start = device // middle_devices * middle_devices * block_rows
    middle_pos = (
        middle_start
        + middle_level_offsets[:, None]
        + DILATION_SECOND * jnp.arange(middle_key_value.shape[1], dtype=jnp.int32)[None, :]
    )
    middle_attention, middle_log_sum = attend(
        middle_level[0],
        middle_key_value[0],
        middle_key_value[1],
        middle_pos,
        valid_limit,
        head_count,
    )
    middle_output, middle_level_mass, middle_selected = scatter_rows(
        middle_attention, middle_log_sum, DILATION_SECOND, middle_level_offsets
    )
    distant_offsets = head_indices % DILATION_THIRD
    distant_local_rows = select_rows(projected_rows, DILATION_THIRD, distant_offsets)
    distant_key_value = lax.all_gather(distant_local_rows[1:], "seq", axis=1, tiled=True)
    distant_positions = (
        distant_offsets[:, None]
        + DILATION_THIRD * jnp.arange(distant_key_value.shape[1], dtype=jnp.int32)[None, :]
    )
    distant_attention, distant_log_sum = attend(
        distant_local_rows[0],
        distant_key_value[0],
        distant_key_value[1],
        distant_positions,
        valid_limit,
        head_count,
    )
    distant_output, distant_mass, distant_selected = scatter_rows(
        distant_attention, distant_log_sum, DILATION_THIRD, distant_offsets
    )
    outputs = jnp.stack([near_out, middle_output, distant_output])
    masses = jnp.stack([near_mass, middle_level_mass, distant_mass])
    selects = jnp.stack([near_sel, middle_selected, distant_selected])
    ceiling = jnp.max(masses, axis=0)
    shares = jnp.where(selects, jnp.exp(masses - ceiling), 0.0)
    combined = jnp.sum(shares[..., None] * outputs, axis=0) / jnp.sum(shares, axis=0)[..., None]
    combined = jnp.where((row_index < valid_limit)[:, None, None], combined, 0.0).reshape(
        block_rows, cols_here
    )
    row_total, row_square = lax.psum(
        (jnp.sum(combined, axis=1), jnp.sum(combined * combined, axis=1)), "head"
    )
    mean_value = row_total / DS
    mean_square = row_square / DS
    scaling = lax.rsqrt(mean_square - mean_value * mean_value + layer_eps)
    settled = ((combined - mean_value[:, None]) * scaling[:, None] * sub_gain).astype(jnp.bfloat16)
    partial_rows = jnp.dot(settled, w_out, preferred_element_type=jnp.float32)
    branch_sum = lax.psum_scatter(partial_rows, "head", scatter_dimension=1, tiled=True)
    return own_part.astype(jnp.float32) + branch_sum


def solution(mesh):
    placed = (
        P(("groups", "seq"), None, None),
        P(),
        P(None, "seq", "head"),
        P("head", "seq"),
        P(),
        P(),
        P(None, "head"),
        P("head"),
        P(("groups", "seq"), "head"),
        P("groups"),
        P("groups"),
        P(),
        P(None, None, "head"),
        P("head"),
        P("head", None),
    )
    return jax.shard_map(
        body, mesh=mesh, in_specs=placed, out_specs=P(("groups", "seq"), "head"), check_vma=False
    )
```

profile of v0, /device:TPU:0, one launch (start us, length us, event | category | flops | bytes accessed | tf_op | source)
XLA Modules:
  0.0 281.4 jit_solution(12463239555199441893)
XLA Ops:
  6.6 0.7 all-gather.3.cloned.1.call-update
  7.3 2.0 convert_reduce_fusion.1
  10.5 4.3 %scatter_custom_fusion = s32[1024]{0:T(1024)S(1)} fusion(s32[1024]{0:T(1024)S(1)} %compare_select_fusion, s32[1024]{0:T(1024)S(1)} %iota.73, s32[]{:T(128)} %constant.151.clone.1), kind=kCustom, calls=%fused_computation.103 | custom fusion | bytes 4100 | tf_op jit(solution)/shard_map/scatter | solution.py:123
  15.6 1.7 fusion.4
  17.3 109.7 %all-gather.3.cloned.1.call-done = bf16[2,1536,1024]{2,1,0:T(8,128)(2,1)} async-done(((bf16[2,384,1024]{2,1,0:T(8,128)(2,1)}), bf16[2,1536,1024]{2,1,0:T(8,128)(2,1)}) %all-gather.3.cloned.1.call-update) | async-done | bytes 6291472 | tf_op jit(solution)/shard_map/all_gather | solution.py:98
  127.0 6.0 %convolution_bitcast_fusion = f32[2,512,1024]{2,1,0:T(8,128)S(1)} fusion(bf16[2,1536,1024]{2,1,0:T(8,128)(2,1)} %all-gather.3.cloned.1.call-done, bf16[512,1536]{1,0:T(8,128)(2,1)} %fusion.4), kind=kOutput, calls=%fused_computation.14 | convolution fusion | flops 3221225472 | bytes 12058624 | tf_op jit(solution)/shard_map/rk,gkf->grf/dot_general | solution.py:95
  133.0 0.6 fusion.51
  133.6 0.6 convert_reduce_fusion.2
  134.2 13.2 %all-gather = f32[4,2,1024]{2,1,0:T(2,128)S(1)} all-gather(f32[1,2,1024]{2,1,0:T(2,128)S(1)} %multiply_bitcast_fusion), channel_id=1, replica_groups=mesh['groups'=2,'seq'=4,'head'=4] {'seq'}, dimensions={0}, use_global_device_ids=true | all-gather | bytes 40960 | tf_op jit(solution)/shard_map/all_gather | solution.py:105
  147.9 0.6 all_to_all.22
  148.5 3.3 %all-to-all-start = ((f32[4,2,384]{2,1,0:T(2,128)}), f32[4,2,384]{2,1,0:T(2,128)S(1)}, u32[]{:S(2)}, u32[]{:S(2)}) async-start(f32[4,2,384]{2,1,0:T(2,128)} %all_to_all.22), calls=%async_computation | async-start | bytes 24576 | tf_op jit(solution)/shard_map/all_to_all | solution.py:107
  151.8 5.6 %all-to-all-done = f32[4,2,384]{2,1,0:T(2,128)S(1)} async-done(((f32[4,2,384]{2,1,0:T(2,128)}), f32[4,2,384]{2,1,0:T(2,128)S(1)}, u32[]{:S(2)}, u32[]{:S(2)}) %all-to-all-start) | async-done | bytes 12320 | tf_op jit(solution)/shard_map/all_to_all | solution.py:107
  157.3 10.1 %psum.21 = f32[2,1536]{1,0:T(2,128)S(1)} all-reduce(f32[2,1536]{1,0:T(2,128)S(1)} %bitcast.134), channel_id=1, replica_groups=mesh['groups'=2,'seq'=4,'head'=4] {'head'}, use_global_device_ids=true, to_apply=%region_7.8 | all-reduce | flops 3072 | bytes 24576 | tf_op jit(solution)/shard_map/psum | solution.py:108
  168.5 0.8 copy.71
  169.3 3.3 %all-to-all-start.1 = ((bf16[4,64,192]{2,1,0:T(8,128)(2,1)}), bf16[4,64,192]{2,1,0:T(8,128)(2,1)S(1)}, u32[]{:S(2)}, u32[]{:S(2)}) async-start(bf16[4,64,192]{2,1,0:T(8,128)(2,1)} %bitcast.8), calls=%async_computation.1 | async-start | bytes 262144 | tf_op jit(solution)/shard_map/all_to_all | solution.py:131
  173.4 5.2 %all-to-all-done.1 = bf16[4,64,192]{2,1,0:T(8,128)(2,1)S(1)} async-done(((bf16[4,64,192]{2,1,0:T(8,128)(2,1)}), bf16[4,64,192]{2,1,0:T(8,128)(2,1)S(1)}, u32[]{:S(2)}, u32[]{:S(2)}) %all-to-all-start.1) | async-done | bytes 98336 | tf_op jit(solution)/shard_map/all_to_all | solution.py:131
  178.6 1.2 gather_fusion
  179.9 6.4 %all_gather.17 = bf16[256,768]{0,1:T(8,128)(2,1)S(1)} all-gather(bf16[256,192]{0,1:T(8,128)(2,1)S(1)} %broadcast_select_fusion.2), channel_id=1, replica_groups=mesh['groups'=2,'seq'=4,'head'=4] {'head'}, dimensions={1}, use_global_device_ids=true | all-gather | bytes 491520 | tf_op jit(solution)/shard_map/all_gather | solution.py:137
  187.8 0.7 select_reduce_fusion.1
  188.8 14.0 %all_gather.18 = bf16[2,256,192]{2,0,1:T(2,128)(2,1)S(1)} all-gather(bf16[2,64,192]{2,0,1:T(2,128)(2,1)S(1)} %copy.79), channel_id=1, replica_groups=mesh['groups'=2,'seq'=4,'head'=4] {'seq'}, dimensions={1}, use_global_device_ids=true | all-gather | bytes 245760 | tf_op jit(solution)/shard_map/all_gather | solution.py:170
  204.8 0.6 select_reduce_fusion
  205.5 13.3 %all_gather.19 = bf16[2,64,192]{2,1,0:T(8,128)(2,1)S(1)} all-gather(bf16[2,16,192]{2,1,0:T(8,128)(2,1)S(1)} %slice.61), channel_id=1, replica_groups=mesh['groups'=2,'seq'=4,'head'=4] {'seq'}, dimensions={1}, use_global_device_ids=true | all-gather | bytes 61440 | tf_op jit(solution)/shard_map/all_gather | solution.py:194
  221.1 6.2 %collective-permute-done = bf16[2,256,192]{1,2,0:T(8,128)(2,1)S(1)} collective-permute-done((bf16[2,256,192]{1,2,0:T(8,128)(2,1)S(1)}, bf16[2,256,192]{1,2,0:T(8,128)(2,1)S(1)}, u32[]{:S(2)}, u32[]{:S(2)}) %collective-permute-start) | collective-permute-done | bytes 196640 | tf_op jit(solution)/shard_map/ppermute | solution.py:20
  227.3 0.8 collective-permute-start.1
  228.2 11.7 %collective-permute-done.1 = bf16[2,512,192]{1,2,0:T(8,128)(2,1)S(1)} collective-permute-done((bf16[2,512,192]{1,2,0:T(8,128)(2,1)S(1)}, bf16[2,512,192]{1,2,0:T(8,128)(2,1)S(1)}, u32[]{:S(2)}, u32[]{:S(2)}) %collective-permute-start.1) | collective-permute-done | bytes 393248 | tf_op jit(solution)/shard_map/ppermute | solution.py:20
  240.2 0.9 fusion
  241.0 1.0 fusion.1
  242.1 1.2 fusion.8
  243.6 5.7 %all-reduce = (f32[256]{0:T(256)S(1)}, f32[256]{0:T(256)S(1)}) all-reduce(f32[256]{0:T(256)S(1)} %get-tuple-element.8, f32[256]{0:T(256)S(1)} %get-tuple-element.7), channel_id=1, replica_groups=mesh['groups'=2,'seq'=4,'head'=4] {'head'}, use_global_device_ids=true, to_apply=%region_25.26 | all-reduce | flops 512 | bytes 4096 | tf_op jit(solution)/shard_map/psum | solution.py:219
  249.4 1.2 fusion.58
  250.6 22.4 %reduce-scatter.2.cloned.1.call-done = f32[256,192]{0,1:T(8,128)} async-done(((f32[256,768]{0,1:T(8,128)}), f32[256,192]{0,1:T(8,128)}) %reduce-scatter.2.cloned.1.call-update) | async-done | bytes 196624 | tf_op jit(solution)/shard_map/reduce_scatter | solution.py:227
  273.0 1.6 convert_add_fusion
  (135 shorter events, 10.3 us)
Async XLA Ops:
  6.5 180.1 %copy-start = (bf16[3,768,192]{1,2,0:T(8,128)(2,1)S(1)}, bf16[3,768,192]{1,2,0:T(8,128)(2,1)}, u32[]{:S(2)}) copy-start(bf16[3,768,192]{1,2,0:T(8,128)(2,1)} %param.27) | copy-start | bytes 2654212
  6.5 2.7 copy-start.1
  6.5 4.0 %copy-start.7 = (s32[1024]{0:T(1024)S(1)}, s32[1024]{0:T(1024)}, u32[]{:S(2)}) copy-start(s32[1024]{0:T(1024)} %param.24) | copy-start | bytes 12292
  6.5 9.1 %copy-start.5 = (f32[1536]{0:T(1024)S(1)}, f32[1536]{0:T(1024)}, u32[]{:S(2)}) copy-start(f32[1536]{0:T(1024)} %param.16) | copy-start | bytes 18436
  6.5 120.5 %all-gather.3.cloned.1.call-start = ((), (), s32[]{:S(2)}) async-start(), calls=%async_computation.3 | async-start | bytes 7864320 | tf_op jit(solution)/shard_map/all_gather | solution.py:98
  133.6 13.9 %copy-start.3 = (bf16[1024,384]{1,0:T(8,128)(2,1)S(1)}, bf16[1024,384]{1,0:T(8,128)(2,1)}, u32[]{:S(2)}) copy-start(bf16[1024,384]{1,0:T(8,128)(2,1)} %param.18) | copy-start | bytes 2359300
  133.6 33.9 %copy-start.6 = (f32[1536]{0:T(1024)S(1)}, f32[1536]{0:T(1024)}, u32[]{:S(2)}) copy-start(f32[1536]{0:T(1024)} %param.19) | copy-start | bytes 18436
  133.6 34.2 %copy-start.9 = (bf16[1536,192]{0,1:T(8,128)(2,1)S(1)}, bf16[1536,192]{0,1:T(8,128)(2,1)}, u32[]{:S(2)}) copy-start(bf16[1536,192]{0,1:T(8,128)(2,1)} %param.21) | copy-start | bytes 1769476
  133.6 34.2 %copy-start.11 = (f32[1536]{0:T(1024)S(1)}, f32[1536]{0:T(1024)}, u32[]{:S(2)}) copy-start(f32[1536]{0:T(1024)} %param.20) | copy-start | bytes 18436
  133.6 34.2 %copy-start.13 = (f32[192]{0:T(256)S(1)}, f32[192]{0:T(256)}, u32[]{:S(2)}) copy-start(f32[192]{0:T(256)} %param.22) | copy-start | bytes 2308
  133.6 34.7 %copy-start.10 = (bf16[254,192]{0,1:T(8,128)(2,1)S(1)}, bf16[254,192]{0,1:T(8,128)(2,1)}, u32[]{:S(2)}) copy-start(bf16[254,192]{0,1:T(8,128)(2,1)} %param.23) | copy-start | bytes 292612
  134.2 52.4 %copy-start.12 = (f32[768]{0:T(1024)S(1)}, f32[768]{0:T(1024)}, u32[]{:S(2)}) copy-start(f32[768]{0:T(1024)} %param.26) | copy-start | bytes 9220
  148.5 8.8 %all-to-all-start = ((f32[4,2,384]{2,1,0:T(2,128)}), f32[4,2,384]{2,1,0:T(2,128)S(1)}, u32[]{:S(2)}, u32[]{:S(2)}) async-start(f32[4,2,384]{2,1,0:T(2,128)} %all_to_all.22), calls=%async_computation | async-start | bytes 24576 | tf_op jit(solution)/shard_map/all_to_all | solution.py:107
  169.3 9.4 %all-to-all-start.1 = ((bf16[4,64,192]{2,1,0:T(8,128)(2,1)}), bf16[4,64,192]{2,1,0:T(8,128)(2,1)S(1)}, u32[]{:S(2)}, u32[]{:S(2)}) async-start(bf16[4,64,192]{2,1,0:T(8,128)(2,1)} %bitcast.8), calls=%async_computation.1 | async-start | bytes 262144 | tf_op jit(solution)/shard_map/all_to_all | solution.py:131
  172.6 100.4 %reduce-scatter.2.cloned.1.call-start = ((), (), s32[]{:S(2)}) async-start(), calls=%async_computation.4 | async-start | bytes 983040 | tf_op jit(solution)/shard_map/reduce_scatter | solution.py:227
  187.2 16.6 %copy-start.2 = (bf16[3,256,192]{1,2,0:T(8,128)(2,1)}, bf16[3,256,192]{1,2,0:T(8,128)(2,1)S(1)}, u32[]{:S(2)}) copy-start(bf16[3,256,192]{1,2,0:T(8,128)(2,1)S(1)} %convert_bitcast_fusion) | copy-start | bytes 884740
  219.6 7.7 %collective-permute-start = (bf16[2,256,192]{1,2,0:T(8,128)(2,1)S(1)}, bf16[2,256,192]{1,2,0:T(8,128)(2,1)S(1)}, u32[]{:S(2)}, u32[]{:S(2)}) collective-permute-start(bf16[2,256,192]{1,2,0:T(8,128)(2,1)S(1)} %slice.71), channel_id=1, source_target_pairs={{0,4},{4,0},{8,12},{12,8},{1,5},{5,1},{9,13},{13,9},{2,6},{6,2},{1... | collective-permute-start | bytes 589832 | tf_op jit(solution)/shard_map/ppermute | solution.py:20
  220.5 19.7 %slice-start = ((bf16[3,256,192]{1,2,0:T(8,128)(2,1)}), bf16[1,256,192]{1,2,0:T(8,128)(2,1)S(1)}, s32[]{:S(2)}) async-start(bf16[3,256,192]{1,2,0:T(8,128)(2,1)} %copy-done.2), calls=%async_computation.5 | async-start | bytes 196608 | tf_op jit(solution)/shard_map/slice | solution.py:163
  227.3 12.5 %collective-permute-start.1 = (bf16[2,512,192]{1,2,0:T(8,128)(2,1)S(1)}, bf16[2,512,192]{1,2,0:T(8,128)(2,1)S(1)}, u32[]{:S(2)}, u32[]{:S(2)}) collective-permute-start(bf16[2,512,192]{1,2,0:T(8,128)(2,1)S(1)} %maximum_select_fusion.1), channel_id=1, source_target_pairs={{0,8},{4,12},{8,0},{12,4},{1,9},{5,13},{9,1},{13,5},{2,10},{6,14},... | collective-permute-start | bytes 1179656 | tf_op jit(solution)/shard_map/ppermute | solution.py:20
  242.1 7.2 %copy-start.8 = (f32[192]{0:T(256)S(1)}, f32[192]{0:T(256)}, u32[]{:S(2)}) copy-start(f32[192]{0:T(256)} %param.28) | copy-start | bytes 2308
  242.1 7.3 %copy-start.4 = (bf16[192,768]{1,0:T(8,128)(2,1)S(1)}, bf16[192,768]{1,0:T(8,128)(2,1)}, u32[]{:S(2)}) copy-start(bf16[192,768]{1,0:T(8,128)(2,1)} %param.29) | copy-start | bytes 884740
Sparse Core Ops, SparseCore 0:
  8.9 118.0 all-gather.2
  250.7 22.2 reduce-scatter.1
where the time goes:
time: 282 us; the launch traced here: 281 us
  waiting for transfers between devices  161 us (57%)
  blocking collectives  62.7 us (22%)
  between operations  14.7 us (5%)
  local copies, waits for them, and re-layouts  12.1 us (4%)
  matrix products  11.7 us (4%)
  other arithmetic  11.2 us (4%)
  starting transfers between devices  7.51 us (3%)
    all_gather x1, waiting for transfers between devices, body(): lax.all_gather(w_gate_up, 'seq', axis=1, tiled=True)  110 us
    reduce_scatter x1, waiting for transfers between devices, body(): lax.psum_scatter(partial_rows, 'head', scatter_dimension=1, tiled=True)  22.4 us
    ppermute x2, waiting for transfers between devices, from_partner(): return lax.ppermute(value, axis, pairs)  17.9 us
    all_gather x1, blocking collectives, body(): every_row = lax.all_gather(middle_key_value, 'seq', axis=1, tiled=True)  14 us
    all_gather x1, blocking collectives, body(): lax.all_gather(distant_local_rows[1:], 'seq', axis=1, tiled=True)  13.3 us
    all_gather x1, blocking collectives, body(): everyone = lax.all_gather(pooled_hidden, 'seq', axis=0, tiled=True)  13.2 us
    psum x1, blocking collectives, body(): summed = lax.psum(pooled_part, 'head')  10.1 us
    all_gather x1, blocking collectives, body(): sequence = lax.all_gather(own_part, 'head', axis=1, tiled=True)  6.37 us
  transfers between devices with their start and end apart: 6, of which 6 were waited for; matrix products, arithmetic and copies ran while one was open for 4% of the time, Pallas kernels for 0%

commit v1 on v0

--- a/solution.py
+++ b/solution.py
@@ -92,12 +92,37 @@
     token_rows = tile_tokens.reshape(new_count * patch_count, tile_width)
     normed = normalize(token_rows.astype(jnp.float32), tile_gain).astype(jnp.bfloat16)
     hidden_width = w_gate_up.shape[2]
+    devices, mine, rows = (lax.axis_size("seq"), lax.axis_index("seq"), w_gate_up.shape[1])
+    right = [(i, (i + 1) % devices) for i in range(devices)]
+    left = [(i, (i - 1) % devices) for i in range(devices)]
+    middle = devices // 2
+    from_left = from_right = w_gate_up
     gate_up = jnp.einsum(
         "rk,gkf->grf",
-        normed,
-        lax.all_gather(w_gate_up, "seq", axis=1, tiled=True),
+        lax.dynamic_slice_in_dim(normed, mine * rows, w_gate_up.shape[1], axis=1),
+        w_gate_up,
         preferred_element_type=jnp.float32,
     )
+    for step in range(1, middle + 1):
+        from_left = lax.ppermute(from_left, "seq", right)
+        if step < devices - middle:
+            from_right = lax.ppermute(from_right, "seq", left)
+            gate_up = gate_up + jnp.einsum(
+                "rk,gkf->grf",
+                lax.dynamic_slice_in_dim(
+                    normed, (mine + step) % devices * rows, from_right.shape[1], axis=1
+                ),
+                from_right,
+                preferred_element_type=jnp.float32,
+            )
+        gate_up = gate_up + jnp.einsum(
+            "rk,gkf->grf",
+            lax.dynamic_slice_in_dim(
+                normed, (mine - step) % devices * rows, from_left.shape[1], axis=1
+            ),
+            from_left,
+            preferred_element_type=jnp.float32,
+        )
     hidden = (jax.nn.silu(gate_up[0]) * gate_up[1]).astype(jnp.bfloat16)
     pooled_hidden = jnp.mean(
         hidden.reshape(new_count, patch_count, hidden_width), axis=1, dtype=jnp.float32

time: 282 us -> 265 us (0.940)
  waiting for transfers between devices: 161 us -> 135 us
  starting transfers between devices: 7.51 us -> 12.9 us
    all_gather x1 -> x0, waiting for transfers between devices: 110 us -> none  [body(): lax.all_gather(w_gate_up, 'seq', axis=1, tiled=True)]
    ppermute x0 -> x3, waiting for transfers between devices: none -> 83.7 us  [the longest x2 55.7 us: body(): from_left = lax.ppermute(from_left, 'seq', right)]
    ppermute x0 -> x3, starting transfers between devices: none -> 5.14 us  [the longest x2 3.05 us: body(): from_left = lax.ppermute(from_left, 'seq', right)]
    dot_general x1 -> x4, matrix products: 5.96 us -> 8.01 us  [the longest x2 4.08 us: body(): jnp.einsum('rk,gkf->grf', lax.dynamic_slice_in_dim(normed, (mine - step)...]
  transfers between devices with their start and end apart: 6 -> 8, of which waited for: 6 -> 8; matrix products, arithmetic and copies ran while one was open for 4% -> 7% of each run, Pallas kernels for 0% -> 0%
where the time goes in v1:
time: 265 us; the launch traced here: 264 us
  waiting for transfers between devices  135 us (51%)
  blocking collectives  63 us (24%)
  between operations  14.8 us (6%)
  matrix products  13.7 us (5%)
  starting transfers between devices  12.9 us (5%)
  other arithmetic  12.9 us (5%)
  local copies, waits for them, and re-layouts  12.1 us (5%)
    ppermute x2, waiting for transfers between devices, body(): from_left = lax.ppermute(from_left, 'seq', right)  55.7 us
    ppermute x1, waiting for transfers between devices, body(): from_right = lax.ppermute(from_right, 'seq', left)  28 us
    reduce_scatter x1, waiting for transfers between devices, body(): lax.psum_scatter(partial_rows, 'head', scatter_dimension=1, tiled=True)  22.8 us
    ppermute x2, waiting for transfers between devices, from_partner(): return lax.ppermute(value, axis, pairs)  17.7 us
    all_gather x1, blocking collectives, body(): every_row = lax.all_gather(middle_key_value, 'seq', axis=1, tiled=True)  14.4 us
    all_gather x1, blocking collectives, body(): everyone = lax.all_gather(pooled_hidden, 'seq', axis=0, tiled=True)  13.2 us
    all_gather x1, blocking collectives, body(): lax.all_gather(distant_local_rows[1:], 'seq', axis=1, tiled=True)  13.1 us
    psum x1, blocking collectives, body(): summed = lax.psum(pooled_part, 'head')  10.1 us
  transfers between devices with their start and end apart: 8, of which 8 were waited for; matrix products, arithmetic and copies ran while one was open for 7% of the time, Pallas kernels for 0%

profile of v1, /device:TPU:0, one launch (start us, length us, event | category | flops | bytes accessed | tf_op | source)
XLA Modules:
  0.0 264.3 jit_solution(5176897160075647201)
XLA Ops:
  6.5 3.1 %collective-permute-start.1 = (bf16[2,384,1024]{2,1,0:T(8,128)(2,1)}, bf16[2,384,1024]{2,1,0:T(8,128)(2,1)}, u32[]{:S(2)}, u32[]{:S(2)}) collective-permute-start(bf16[2,384,1024]{2,1,0:T(8,128)(2,1)} %param.17), channel_id=1, source_target_pairs={{0,4},{4,8},{8,12},{12,0},{1,5},{5,9},{9,13},{13,1},{2,6},{6,10},{... | collective-permute-start | bytes 4718600 | tf_op jit(solution)/shard_map/ppermute | solution.py:107
  9.6 2.1 collective-permute-start
  13.1 2.0 convert_reduce_fusion.1
  15.1 4.3 %scatter_custom_fusion = s32[1024]{0:T(1024)S(1)} fusion(s32[1024]{0:T(1024)S(1)} %compare_select_fusion, s32[1024]{0:T(1024)S(1)} %iota.73, s32[]{:T(128)} %constant.167.clone.1), kind=kCustom, calls=%fused_computation.113 | custom fusion | bytes 4100 | tf_op jit(solution)/shard_map/scatter | solution.py:148
  20.5 2.0 multiply_reduce_fusion
  22.8 24.4 %collective-permute-done.1 = bf16[2,384,1024]{2,1,0:T(8,128)(2,1)} collective-permute-done((bf16[2,384,1024]{2,1,0:T(8,128)(2,1)}, bf16[2,384,1024]{2,1,0:T(8,128)(2,1)}, u32[]{:S(2)}, u32[]{:S(2)}) %collective-permute-start.1) | collective-permute-done | bytes 1572896 | tf_op jit(solution)/shard_map/ppermute | solution.py:107
  47.8 1.3 fusion.23
  49.1 2.7 %fusion.19 = f32[512,2,1024]{2,0,1:T(8,128)S(1)} fusion(bf16[2,384,1024]{2,1,0:T(8,128)(2,1)} %collective-permute-done.1, bf16[512,1536]{1,0:T(8,128)(2,1)S(1)} %fusion.4, s32[]{:T(128)S(6)} %select_n.209), kind=kOutput, calls=%fused_computation.43 | convolution fusion | flops 805306368 | bytes 6160388 | tf_op jit(solution)/shard_map/rk,gkf->grf/dot_general | solution.py:118
  51.7 28.0 %collective-permute-done = bf16[2,384,1024]{2,1,0:T(8,128)(2,1)} collective-permute-done((bf16[2,384,1024]{2,1,0:T(8,128)(2,1)}, bf16[2,384,1024]{2,1,0:T(8,128)(2,1)}, u32[]{:S(2)}, u32[]{:S(2)}) %collective-permute-start) | collective-permute-done | bytes 1572896 | tf_op jit(solution)/shard_map/ppermute | solution.py:109
  79.7 2.7 %fusion.21 = f32[512,2,1024]{2,0,1:T(8,128)S(1)} fusion(bf16[2,384,1024]{2,1,0:T(8,128)(2,1)} %collective-permute-done, bf16[512,1536]{1,0:T(8,128)(2,1)S(1)} %fusion.4, s32[]{:T(128)S(6)} %select_n.207), kind=kOutput, calls=%fused_computation.45 | convolution fusion | flops 805306368 | bytes 6160388 | tf_op jit(solution)/shard_map/rk,gkf->grf/dot_general | solution.py:110
  82.4 31.3 %collective-permute-done.2 = bf16[2,384,1024]{2,1,0:T(8,128)(2,1)S(1)} collective-permute-done((bf16[2,384,1024]{2,1,0:T(8,128)(2,1)}, bf16[2,384,1024]{2,1,0:T(8,128)(2,1)S(1)}, u32[]{:S(2)}, u32[]{:S(2)}) %collective-permute-start.2) | collective-permute-done | bytes 1572896 | tf_op jit(solution)/shard_map/ppermute | solution.py:107
  113.7 1.4 add_bitcast_fusion
  116.3 13.2 %all-gather = f32[4,2,1024]{2,1,0:T(2,128)S(1)} all-gather(f32[1,2,1024]{2,1,0:T(2,128)S(1)} %multiply_bitcast_fusion), channel_id=1, replica_groups=mesh['groups'=2,'seq'=4,'head'=4] {'seq'}, dimensions={0}, use_global_device_ids=true | all-gather | bytes 40960 | tf_op jit(solution)/shard_map/all_gather | solution.py:130
  130.5 3.3 %all-to-all-start = ((f32[4,2,384]{2,1,0:T(2,128)}), f32[4,2,384]{2,1,0:T(2,128)S(1)}, u32[]{:S(2)}, u32[]{:S(2)}) async-start(f32[4,2,384]{2,1,0:T(2,128)} %all_to_all.22), calls=%async_computation | async-start | bytes 24576 | tf_op jit(solution)/shard_map/all_to_all | solution.py:132
  133.8 5.6 %all-to-all-done = f32[4,2,384]{2,1,0:T(2,128)S(1)} async-done(((f32[4,2,384]{2,1,0:T(2,128)}), f32[4,2,384]{2,1,0:T(2,128)S(1)}, u32[]{:S(2)}, u32[]{:S(2)}) %all-to-all-start) | async-done | bytes 12320 | tf_op jit(solution)/shard_map/all_to_all | solution.py:132
  139.4 10.1 %psum.21 = f32[2,1536]{1,0:T(2,128)S(1)} all-reduce(f32[2,1536]{1,0:T(2,128)S(1)} %bitcast.147), channel_id=1, replica_groups=mesh['groups'=2,'seq'=4,'head'=4] {'head'}, use_global_device_ids=true, to_apply=%region_7.8 | all-reduce | flops 3072 | bytes 24576 | tf_op jit(solution)/shard_map/psum | solution.py:133
  151.3 3.3 %all-to-all-start.1 = ((bf16[4,64,192]{2,1,0:T(8,128)(2,1)}), bf16[4,64,192]{2,1,0:T(8,128)(2,1)S(1)}, u32[]{:S(2)}, u32[]{:S(2)}) async-start(bf16[4,64,192]{2,1,0:T(8,128)(2,1)} %bitcast.11), calls=%async_computation.1 | async-start | bytes 262144 | tf_op jit(solution)/shard_map/all_to_all | solution.py:156
  155.5 5.2 %all-to-all-done.1 = bf16[4,64,192]{2,1,0:T(8,128)(2,1)S(1)} async-done(((bf16[4,64,192]{2,1,0:T(8,128)(2,1)}), bf16[4,64,192]{2,1,0:T(8,128)(2,1)S(1)}, u32[]{:S(2)}, u32[]{:S(2)}) %all-to-all-start.1) | async-done | bytes 98336 | tf_op jit(solution)/shard_map/all_to_all | solution.py:156
  160.7 1.2 gather_fusion
  162.0 6.5 %all_gather.13 = bf16[256,768]{0,1:T(8,128)(2,1)S(1)} all-gather(bf16[256,192]{0,1:T(8,128)(2,1)S(1)} %broadcast_select_fusion.2), channel_id=1, replica_groups=mesh['groups'=2,'seq'=4,'head'=4] {'head'}, dimensions={1}, use_global_device_ids=true | all-gather | bytes 491520 | tf_op jit(solution)/shard_map/all_gather | solution.py:162
  170.8 13.1 %all_gather.15 = bf16[2,64,192]{2,1,0:T(8,128)(2,1)S(1)} all-gather(bf16[2,16,192]{2,1,0:T(8,128)(2,1)S(1)} %slice.61), channel_id=1, replica_groups=mesh['groups'=2,'seq'=4,'head'=4] {'seq'}, dimensions={1}, use_global_device_ids=true | all-gather | bytes 61440 | tf_op jit(solution)/shard_map/all_gather | solution.py:219
  186.2 14.4 %all_gather.14 = bf16[2,256,192]{2,0,1:T(2,128)(2,1)S(1)} all-gather(bf16[2,64,192]{2,0,1:T(2,128)(2,1)S(1)} %copy.79), channel_id=1, replica_groups=mesh['groups'=2,'seq'=4,'head'=4] {'seq'}, dimensions={1}, use_global_device_ids=true | all-gather | bytes 245760 | tf_op jit(solution)/shard_map/all_gather | solution.py:195
  203.5 6.1 %collective-permute-done.3 = bf16[2,256,192]{1,2,0:T(8,128)(2,1)S(1)} collective-permute-done((bf16[2,256,192]{1,2,0:T(8,128)(2,1)S(1)}, bf16[2,256,192]{1,2,0:T(8,128)(2,1)S(1)}, u32[]{:S(2)}, u32[]{:S(2)}) %collective-permute-start.3) | collective-permute-done | bytes 196640 | tf_op jit(solution)/shard_map/ppermute | solution.py:20
  209.7 1.1 collective-permute-start.4
  210.8 11.6 %collective-permute-done.4 = bf16[2,512,192]{1,2,0:T(8,128)(2,1)S(1)} collective-permute-done((bf16[2,512,192]{1,2,0:T(8,128)(2,1)S(1)}, bf16[2,512,192]{1,2,0:T(8,128)(2,1)S(1)}, u32[]{:S(2)}, u32[]{:S(2)}) %collective-permute-start.4) | collective-permute-done | bytes 393248 | tf_op jit(solution)/shard_map/ppermute | solution.py:20
  222.6 0.9 fusion
  223.5 1.0 fusion.1
  224.6 1.2 fusion.7
  226.0 5.7 %all-reduce = (f32[256]{0:T(256)S(1)}, f32[256]{0:T(256)S(1)}) all-reduce(f32[256]{0:T(256)S(1)} %get-tuple-element.8, f32[256]{0:T(256)S(1)} %get-tuple-element.7), channel_id=1, replica_groups=mesh['groups'=2,'seq'=4,'head'=4] {'head'}, use_global_device_ids=true, to_apply=%region_25.26 | all-reduce | flops 512 | bytes 4096 | tf_op jit(solution)/shard_map/psum | solution.py:244
  231.8 1.2 fusion.72
  233.1 22.8 %reduce-scatter.2.cloned.1.call-done = f32[256,192]{0,1:T(8,128)} async-done(((f32[256,768]{0,1:T(8,128)}), f32[256,192]{0,1:T(8,128)}) %reduce-scatter.2.cloned.1.call-update) | async-done | bytes 196624 | tf_op jit(solution)/shard_map/reduce_scatter | solution.py:252
  255.8 1.6 convert_add_fusion
  (141 shorter events, 15.5 us)
Async XLA Ops:
  6.5 162.3 %copy-start = (bf16[3,768,192]{1,2,0:T(8,128)(2,1)S(1)}, bf16[3,768,192]{1,2,0:T(8,128)(2,1)}, u32[]{:S(2)}) copy-start(bf16[3,768,192]{1,2,0:T(8,128)(2,1)} %param.27) | copy-start | bytes 2654212
  6.5 40.7 %copy-start.1 = (bf16[2,256,1536]{2,1,0:T(8,128)(2,1)S(1)}, bf16[2,256,1536]{2,1,0:T(8,128)(2,1)}, u32[]{:S(2)}) copy-start(bf16[2,256,1536]{2,1,0:T(8,128)(2,1)} %param.15) | copy-start | bytes 4718596
  6.5 40.7 %copy-start.6 = (f32[1536]{0:T(1024)S(1)}, f32[1536]{0:T(1024)}, u32[]{:S(2)}) copy-start(f32[1536]{0:T(1024)} %param.16) | copy-start | bytes 18436
  6.5 40.7 %collective-permute-start.1 = (bf16[2,384,1024]{2,1,0:T(8,128)(2,1)}, bf16[2,384,1024]{2,1,0:T(8,128)(2,1)}, u32[]{:S(2)}, u32[]{:S(2)}) collective-permute-start(bf16[2,384,1024]{2,1,0:T(8,128)(2,1)} %param.17), channel_id=1, source_target_pairs={{0,4},{4,8},{8,12},{12,0},{1,5},{5,9},{9,13},{13,1},{2,6},{6,10},{... | collective-permute-start | bytes 4718600 | tf_op jit(solution)/shard_map/ppermute | solution.py:107
  9.6 70.1 %collective-permute-start = (bf16[2,384,1024]{2,1,0:T(8,128)(2,1)}, bf16[2,384,1024]{2,1,0:T(8,128)(2,1)}, u32[]{:S(2)}, u32[]{:S(2)}) collective-permute-start(bf16[2,384,1024]{2,1,0:T(8,128)(2,1)} %param.17), channel_id=1, source_target_pairs={{0,12},{4,0},{8,4},{12,8},{1,13},{5,1},{9,5},{13,9},{2,14},{6,2},{... | collective-permute-start | bytes 4718600 | tf_op jit(solution)/shard_map/ppermute | solution.py:109
  22.8 25.0 %copy-start.3 = (bf16[2,384,1024]{2,1,0:T(8,128)(2,1)S(1)}, bf16[2,384,1024]{2,1,0:T(8,128)(2,1)}, u32[]{:S(2)}) copy-start(bf16[2,384,1024]{2,1,0:T(8,128)(2,1)} %param.17) | copy-start | bytes 4718596
  47.2 66.5 %collective-permute-start.2 = (bf16[2,384,1024]{2,1,0:T(8,128)(2,1)}, bf16[2,384,1024]{2,1,0:T(8,128)(2,1)S(1)}, u32[]{:S(2)}, u32[]{:S(2)}) collective-permute-start(bf16[2,384,1024]{2,1,0:T(8,128)(2,1)} %collective-permute-done.1), channel_id=1, source_target_pairs={{0,4},{4,8},{8,12},{12,0},{1,5},{5,9},{9,13},{13,1},{2,6},{6,10},{... | collective-permute-start | bytes 4718600 | tf_op jit(solution)/shard_map/ppermute | solution.py:107
  115.6 13.9 %copy-start.4 = (bf16[1024,384]{1,0:T(8,128)(2,1)S(1)}, bf16[1024,384]{1,0:T(8,128)(2,1)}, u32[]{:S(2)}) copy-start(bf16[1024,384]{1,0:T(8,128)(2,1)} %param.18) | copy-start | bytes 2359300
  115.6 33.9 %copy-start.7 = (f32[1536]{0:T(1024)S(1)}, f32[1536]{0:T(1024)}, u32[]{:S(2)}) copy-start(f32[1536]{0:T(1024)} %param.19) | copy-start | bytes 18436
  115.6 34.2 %copy-start.9 = (bf16[1536,192]{0,1:T(8,128)(2,1)S(1)}, bf16[1536,192]{0,1:T(8,128)(2,1)}, u32[]{:S(2)}) copy-start(bf16[1536,192]{0,1:T(8,128)(2,1)} %param.21) | copy-start | bytes 1769476
  115.7 34.2 %copy-start.11 = (f32[1536]{0:T(1024)S(1)}, f32[1536]{0:T(1024)}, u32[]{:S(2)}) copy-start(f32[1536]{0:T(1024)} %param.20) | copy-start | bytes 18436
  115.7 34.2 %copy-start.13 = (f32[192]{0:T(256)S(1)}, f32[192]{0:T(256)}, u32[]{:S(2)}) copy-start(f32[192]{0:T(256)} %param.22) | copy-start | bytes 2308
  115.7 34.6 %copy-start.10 = (bf16[254,192]{0,1:T(8,128)(2,1)S(1)}, bf16[254,192]{0,1:T(8,128)(2,1)}, u32[]{:S(2)}) copy-start(bf16[254,192]{0,1:T(8,128)(2,1)} %param.23) | copy-start | bytes 292612
  116.3 52.5 %copy-start.12 = (f32[768]{0:T(1024)S(1)}, f32[768]{0:T(1024)}, u32[]{:S(2)}) copy-start(f32[768]{0:T(1024)} %param.26) | copy-start | bytes 9220
  130.5 8.8 %all-to-all-start = ((f32[4,2,384]{2,1,0:T(2,128)}), f32[4,2,384]{2,1,0:T(2,128)S(1)}, u32[]{:S(2)}, u32[]{:S(2)}) async-start(f32[4,2,384]{2,1,0:T(2,128)} %all_to_all.22), calls=%async_computation | async-start | bytes 24576 | tf_op jit(solution)/shard_map/all_to_all | solution.py:132
  151.3 9.4 %all-to-all-start.1 = ((bf16[4,64,192]{2,1,0:T(8,128)(2,1)}), bf16[4,64,192]{2,1,0:T(8,128)(2,1)S(1)}, u32[]{:S(2)}, u32[]{:S(2)}) async-start(bf16[4,64,192]{2,1,0:T(8,128)(2,1)} %bitcast.11), calls=%async_computation.1 | async-start | bytes 262144 | tf_op jit(solution)/shard_map/all_to_all | solution.py:156
  154.7 101.2 %reduce-scatter.2.cloned.1.call-start = ((), (), s32[]{:S(2)}) async-start(), calls=%async_computation.3 | async-start | bytes 983040 | tf_op jit(solution)/shard_map/reduce_scatter | solution.py:252
  169.4 16.4 %copy-start.2 = (bf16[3,256,192]{1,2,0:T(8,128)(2,1)}, bf16[3,256,192]{1,2,0:T(8,128)(2,1)S(1)}, u32[]{:S(2)}) copy-start(bf16[3,256,192]{1,2,0:T(8,128)(2,1)S(1)} %convert_bitcast_fusion) | copy-start | bytes 884740
  202.0 7.6 %collective-permute-start.3 = (bf16[2,256,192]{1,2,0:T(8,128)(2,1)S(1)}, bf16[2,256,192]{1,2,0:T(8,128)(2,1)S(1)}, u32[]{:S(2)}, u32[]{:S(2)}) collective-permute-start(bf16[2,256,192]{1,2,0:T(8,128)(2,1)S(1)} %slice.71), channel_id=1, source_target_pairs={{0,4},{4,0},{8,12},{12,8},{1,5},{5,1},{9,13},{13,9},{2,6},{6,2},{1... | collective-permute-start | bytes 589832 | tf_op jit(solution)/shard_map/ppermute | solution.py:20
  203.3 19.4 %slice-start = ((bf16[3,256,192]{1,2,0:T(8,128)(2,1)}), bf16[1,256,192]{1,2,0:T(8,128)(2,1)S(1)}, s32[]{:S(2)}) async-start(bf16[3,256,192]{1,2,0:T(8,128)(2,1)} %copy-done.2), calls=%async_computation.4 | async-start | bytes 196608 | tf_op jit(solution)/shard_map/slice | solution.py:188
  209.7 12.7 %collective-permute-start.4 = (bf16[2,512,192]{1,2,0:T(8,128)(2,1)S(1)}, bf16[2,512,192]{1,2,0:T(8,128)(2,1)S(1)}, u32[]{:S(2)}, u32[]{:S(2)}) collective-permute-start(bf16[2,512,192]{1,2,0:T(8,128)(2,1)S(1)} %maximum_select_fusion.1), channel_id=1, source_target_pairs={{0,8},{4,12},{8,0},{12,4},{1,9},{5,13},{9,1},{13,5},{2,10},{6,14},... | collective-permute-start | bytes 1179656 | tf_op jit(solution)/shard_map/ppermute | solution.py:20
  224.6 7.2 %copy-start.8 = (f32[192]{0:T(256)S(1)}, f32[192]{0:T(256)}, u32[]{:S(2)}) copy-start(f32[192]{0:T(256)} %param.28) | copy-start | bytes 2308
  224.6 7.3 %copy-start.5 = (bf16[192,768]{1,0:T(8,128)(2,1)S(1)}, bf16[192,768]{1,0:T(8,128)(2,1)}, u32[]{:S(2)}) copy-start(bf16[192,768]{1,0:T(8,128)(2,1)} %param.29) | copy-start | bytes 884740
Sparse Core Ops, SparseCore 0:
  233.2 22.6 reduce-scatter.1
